TPU v7x, 256 devices: a whole 4x4x8 slice. The times are simulated.
256 devices in a mesh: gx: 8 (over y, core), gy: 8 (over z), gz: 4 (over x).
Axes of the slice: x: 4, y: 4, z: 8, core: 2. Of those that a mesh axis runs over, the one named last changes fastest.
Arguments:
- blocks: bfloat16 [1536, 64, 4096], P(('gx', 'gy', 'gz')), may hold values from -6 to 6
- ownership: int32 [1536, 3], P(('gx', 'gy', 'gz')), may hold values from -1 to 15, as said below
- basis_rows: bfloat16 [1024, 48], replicated, may hold values from -0.1875 to 0.1875
Outputs:
- gram_matrix: float32 [1024, 1024], P(('gx', 'gy', 'gz'))
Inputs may be any that keep to these rules, and one draw needn't show every extreme that they name: `ownership`: row d * 6 + s is slot s of device d in mesh order. Each row is a block triple (i, j, k) with i <= j <= k, or -1 -1 -1 for an empty slot; every such triple of blocks 0 to 15 stands in exactly one row; the live slots of a device come first; some device has all 6 slots live.
All inputs are finite; a program needn't handle non-finite values.
Results may differ from a plain program's by a relative error of at most 0.0037.
Values may be sent and summed in bfloat16 or wider, within the bound.
A program may use at most 128 MiB of HBM per device.

v0:
```python
import jax
import jax.numpy as jnp
from jax import lax
from jax.sharding import Mesh
from jax.sharding import PartitionSpec as P

N = 1024
NB = 16
R = 48
GX_GY = ("gx_0", "gx_1", "gy")
GX_GY_GZ = ("gx_0", "gx_1", "gy", "gz")


ORDERS = ((0, 1, 2), (0, 2, 1), (1, 0, 2), (1, 2, 0), (2, 0, 1), (2, 1, 0))
REDUCE_FORMS = ("gxyz,gxq->gyzq", "gxyz,gyq->gxzq", "gxyz,gzq->gxyq")


def reduced_to_own(pieces, axes, turns):
    dims = [lax.axis_size(a) for a in axes]
    pieces = pieces.reshape(*dims, *pieces.shape[1:])
    pieces = pieces.transpose(*turns, *range(len(axes), pieces.ndim))
    pieces = pieces.reshape(-1, *pieces.shape[len(axes) :])
    for k in turns:
        pieces = lax.psum_scatter(pieces, axes[k], scatter_dimension=0, tiled=True)
    return pieces[0]


def in_blocks(shard, dim, devices):
    dims = shard.shape
    pieces = shard.reshape(*dims[:dim], devices, dims[dim] // devices, *dims[dim + 1 :])
    return jnp.moveaxis(pieces, dim, 0)


def scatter_axes(shard, axes, turns, dim):
    devices = lax.axis_size(axes)
    return reduced_to_own(in_blocks(shard, dim, devices), axes, turns)


def sent_and_summed(shard, axis, dim):
    pieces = in_blocks(shard, dim, lax.axis_size(axis))
    arrived = lax.all_to_all(pieces, axis, split_axis=0, concat_axis=0, tiled=True)
    return arrived.sum(axis=0)


def unpack(stored, unique_triples):
    number = stored.shape[0]
    extent = stored.shape[1]
    unpacked = stored.reshape(number, extent, extent, extent)
    leading_block_index = lax.broadcasted_iota(jnp.int32, (1, extent, extent, extent), 1)
    middle = lax.broadcasted_iota(jnp.int32, (1, extent, extent, extent), 2)
    trailing = lax.broadcasted_iota(jnp.int32, (1, extent, extent, extent), 3)
    same_front = (unique_triples[:, 0] == unique_triples[:, 1])[:, None, None, None]
    same_back = (unique_triples[:, 1] == unique_triples[:, 2])[:, None, None, None]

    def order_back(values):
        return jnp.where(middle <= trailing, values, jnp.swapaxes(values, 2, 3))

    unpacked = jnp.where(same_back, order_back(unpacked), unpacked)
    unpacked = jnp.where(
        same_front,
        jnp.where(leading_block_index <= middle, unpacked, jnp.swapaxes(unpacked, 1, 2)),
        unpacked,
    )
    unpacked = jnp.where(same_back, order_back(unpacked), unpacked)
    return unpacked


def slot_terms(stored, unique_triples, basis_rows):
    extent = stored.shape[1]
    columns = basis_rows.shape[1]
    unpacked = unpack(stored, unique_triples)
    basis_blocks = basis_rows.reshape(basis_rows.shape[0] // extent, extent, columns)
    selected_rows = jnp.take(
        basis_blocks, jnp.clip(unique_triples, 0, basis_blocks.shape[0] - 1), axis=0
    )
    factors = (selected_rows[:, 0], selected_rows[:, 1], selected_rows[:, 2])
    reduced = [
        jnp.einsum(
            REDUCE_FORMS[slot_pos], unpacked, factors[slot_pos], preferred_element_type=jnp.float32
        ).astype(jnp.bfloat16)
        for slot_pos in range(3)
    ]
    by_row = [0.0, 0.0, 0.0]
    for position in range(6):
        row_slot_index, middle_slot_index, last_slot = ORDERS[position]
        contraction_form = (
            "zixl,zxo->ziol" if row_slot_index < middle_slot_index else "hwie,hwy->hiye"
        )
        contrib = jnp.einsum(
            contraction_form,
            reduced[last_slot],
            factors[middle_slot_index],
            preferred_element_type=jnp.float32,
        )
        ordered = unique_triples[:, jnp.array(ORDERS[position])]
        distinct = unique_triples[:, 0] >= 0
        for earlier in ORDERS[:position]:
            distinct = distinct & jnp.any(ordered != unique_triples[:, jnp.array(earlier)], axis=1)
        by_row[row_slot_index] = by_row[row_slot_index] + jnp.where(
            distinct[:, None, None, None], contrib, 0.0
        )
    stacked = jnp.stack(by_row, axis=1)
    return stacked.reshape(stacked.shape[0], 3, extent, columns * columns)


def local(blocks, ownership, basis_rows):
    slot_total = blocks.shape[0]
    extent = N // NB
    pair_cols = R * R
    per_turn = min(8, slot_total)

    def add_group(batch_index, accumulated):
        first_slot = jnp.minimum(batch_index * per_turn, slot_total - per_turn)
        slot_locations = first_slot + jnp.arange(per_turn, dtype=jnp.int32)
        wanted = (slot_locations >= batch_index * per_turn) & (ownership[:, 0] >= 0)
        contribs = slot_terms(blocks, ownership, basis_rows)
        contribs = jnp.where(wanted[:, None, None, None], contribs, 0.0)
        targets = jnp.clip(ownership, 0, NB - 1).reshape(1, -1)
        onehot = (targets == jnp.arange(NB, dtype=jnp.int32)[:, None]).astype(jnp.float32)
        return accumulated + jnp.einsum(
            "nk,kbc->nbc",
            onehot,
            contribs.reshape(per_turn * 3, extent, pair_cols),
            precision=lax.Precision.HIGHEST,
        )

    zero_rows = jnp.zeros((NB, extent, pair_cols), jnp.float32)
    summed = lax.fori_loop(0, (slot_total + per_turn - 1) // per_turn, add_group, zero_rows)
    partial_value = summed.reshape(N, R, R)
    outgoing_rows = partial_value.reshape(N, pair_cols)
    first_section = scatter_axes(outgoing_rows, GX_GY, (1, 0, 2), 0)
    own_rows = sent_and_summed(first_section, "gz", 0)
    row_block = own_rows.reshape(-1, R, R)
    rounded = (
        (0.5 * (row_block + jnp.swapaxes(row_block, 1, 2)))
        .reshape(-1, pair_cols)
        .astype(jnp.bfloat16)
    )
    gram_rows = lax.dot_general(
        rounded,
        lax.all_gather(rounded, GX_GY_GZ, axis=0, tiled=True),
        (((1,), (1,)), ((), ())),
        preferred_element_type=jnp.float32,
    )
    return gram_rows / R


def solution(mesh):
    split = Mesh(
        mesh.devices.reshape(4, 2, mesh.shape["gy"], mesh.shape["gz"]), ("gx_0", "gx_1", "gy", "gz")
    )
    return jax.shard_map(
        local,
        mesh=split,
        in_specs=(P(GX_GY_GZ, None, None), P(GX_GY_GZ, None), P()),
        out_specs=P(GX_GY_GZ, None),
        check_vma=False,
    )
```

profile of v0, /device:TPU:1, one launch (start us, length us, event | category | flops | bytes accessed | tf_op | source)
XLA Modules:
  0.0 520.9 jit_solution(523102884144031336)
XLA Ops:
  6.8 0.8 compare_bitcast_fusion.2
  7.6 0.7 broadcast_clamp_fusion
  8.3 0.7 compare_and_fusion
  9.0 9.7 %reshape.141 = bf16[6,64,64,64]{3,2,1,0:T(8,128)(2,1)} reshape(bf16[6,64,4096]{2,1,0:T(8,128)(2,1)} %param.23) | data formatting | bytes 6291456 | tf_op jit(solution)/shard_map/while/body/eval_jaxpr/reshape | solution.py:48
  18.7 9.5 %copy.118 = bf16[6,64,64,64]{2,1,3,0:T(8,128)(2,1)} copy(bf16[6,64,64,64]{3,2,1,0:T(8,128)(2,1)} %reshape.141) | data formatting | bytes 6291456 | tf_op jit(solution)/shard_map/while/body/eval_jaxpr/reshape | solution.py:48
  28.2 13.5 %select_select_fusion.2 = bf16[6,64,64,64]{3,1,2,0:T(8,128)(2,1)} fusion(bf16[6,64,64,64]{2,1,3,0:T(8,128)(2,1)} %copy.118, bf16[6,64,64,64]{3,2,1,0:T(8,128)(2,1)} %reshape.141, pred[6]{0:T(512)(128)(4,1)S(1)} %get-tuple-element.73, pred[64,64,64]{2,0,1:T(8,128)(4,1)S(1)} %iota_compare_fusion.1), kind=kLoop, calls=%fused_computation.13 | loop fusion | flops 3145728 | bytes 9699334 | tf_op jit(solution)/shard_map/while/body/eval_jaxpr/jit(_where)/select_n | solution.py:58
  41.7 11.8 %select_select_fusion.1 = bf16[6,64,64,64]{3,1,2,0:T(8,128)(2,1)} fusion(bf16[6,64,64,64]{3,1,2,0:T(8,128)(2,1)} %select_select_fusion.2, pred[6]{0:T(512)(128)(4,1)S(1)} %get-tuple-element.74, pred[64,64,64]{2,0,1:T(8,128)(4,1)S(1)} %iota_compare_fusion), kind=kLoop, calls=%fused_computation.12 | loop fusion | flops 3145728 | bytes 6553606 | tf_op jit(solution)/shard_map/while/body/eval_jaxpr/jit(_where)/select_n | solution.py:59
  53.5 11.9 %copy.122 = bf16[6,64,64,64]{2,1,3,0:T(8,128)(2,1)} copy(bf16[6,64,64,64]{3,1,2,0:T(8,128)(2,1)} %select_select_fusion.1) | data formatting | bytes 6291456 | tf_op jit(solution)/shard_map/while/body/eval_jaxpr/jit(_where)/select_n | solution.py:59
  65.4 15.1 %select_select_fusion = bf16[6,64,64,64]{3,1,2,0:T(8,128)(2,1)} fusion(bf16[6,64,64,64]{2,1,3,0:T(8,128)(2,1)} %copy.122, pred[6]{0:T(512)(128)(4,1)S(1)} %get-tuple-element.73, pred[64,64,64]{2,0,1:T(8,128)(4,1)S(1)} %iota_compare_fusion.1, bf16[6,64,64,64]{3,1,2,0:T(8,128)(2,1)} %select_select_fusion.2, pred[64,64,64]{2,0,1:T(8,128)(4,1)S(1)} %iota_compare_fusion, ...), kind=kLoop, calls=%fused_computation.11 | loop fusion | flops 6291456 | bytes 9961484 | tf_op jit(solution)/shard_map/while/body/eval_jaxpr/jit(_where)/select_n | solution.py:64
  81.0 0.6 gather_fusion
  81.7 4.3 convolution_convert_fusion
  86.0 0.3 slice-done.1
  86.3 7.3 %fusion.21 = bf16[6,64,64,48]{2,3,1,0:T(8,128)(2,1)} fusion(bf16[6,64,64,64]{3,1,2,0:T(8,128)(2,1)S(1)} %bitcast.82, bf16[6,3,64,48]{2,3,0,1:T(8,128)(2,1)S(1)} %copy_select_fusion), kind=kOutput, calls=%fused_computation.34 | convolution fusion | flops 152174592 | bytes 8724480 | tf_op jit(solution)/shard_map/while/body/eval_jaxpr/gxyz,gyq->gxzq/dot_general | solution.py:78
  93.6 4.0 fusion.6
  97.6 7.3 %fusion.8 = f32[6,48,64,48]{2,1,3,0:T(8,128)} fusion(bf16[6,64,64,48]{2,3,1,0:T(8,128)(2,1)S(1)} %convolution_convert_fusion, bf16[6,3,64,48]{2,3,0,1:T(8,128)(2,1)S(1)} %copy_select_fusion), kind=kOutput, calls=%fused_computation.23 | convolution fusion | flops 113246208 | bytes 8331264 | tf_op jit(solution)/shard_map/while/body/eval_jaxpr/zixl,zxo->ziol/dot_general | solution.py:89
  105.0 8.4 %fusion.18 = bf16[6,64,64,48]{2,3,1,0:T(8,128)(2,1)} fusion(bf16[6,64,64,64]{3,1,2,0:T(8,128)(2,1)S(1)} %bitcast.82, bf16[6,3,64,48]{2,3,0,1:T(8,128)(2,1)S(1)} %copy_select_fusion), kind=kOutput, calls=%fused_computation.33 | convolution fusion | flops 152174592 | bytes 8724480 | tf_op jit(solution)/shard_map/while/body/eval_jaxpr/gxyz,gzq->gxyq/dot_general | solution.py:78
  113.4 0.6 gather_fusion.1
  114.0 0.6 gather_fusion.2
  114.6 0.6 gather_fusion.5
  115.2 0.6 gather_fusion.4
  115.7 0.6 gather_fusion.3
  116.3 0.6 gather_fusion.6
  116.9 9.9 %fusion.12 = f32[6,48,64,48]{2,1,3,0:T(8,128)} fusion(bf16[6,64,64,48]{2,3,1,0:T(8,128)(2,1)} %fusion.21, bf16[6,3,64,48]{2,3,0,1:T(8,128)(2,1)S(1)} %copy_select_fusion), kind=kOutput, calls=%fused_computation.27 | convolution fusion | flops 113246208 | bytes 5971968 | tf_op jit(solution)/shard_map/while/body/eval_jaxpr/zixl,zxo->ziol/dot_general | solution.py:89
  126.8 0.5 fusion.35
  127.4 4.9 add_bitcast_fusion
  132.2 9.9 %copy.133 = f32[6,64,48,48]{3,2,1,0:T(8,128)} copy(f32[6,64,48,48]{1,2,3,0:T(8,128)} %add_bitcast_fusion) | data formatting | bytes 7077888 | tf_op jit(solution)/shard_map/while/body/eval_jaxpr/add | solution.py:99
  142.1 7.2 %stack.20 = f32[6,1,64,2304]{3,2,0,1:T(8,128)S(1)} reshape(f32[6,64,48,48]{3,2,1,0:T(8,128)} %copy.133) | data formatting | bytes 7077888 | tf_op jit(solution)/shard_map/while/body/eval_jaxpr/stack | solution.py:102
  149.3 9.1 %add_bitcast_fusion.1 = f32[6,64,48,48]{1,2,3,0:T(8,128)} fusion(f32[6,48,64,48]{2,1,3,0:T(8,128)} %fusion.8, pred[6]{0:T(512)(128)(4,1)} %get-tuple-element.77, pred[6]{0:T(512)(128)(4,1)S(1)} %get-tuple-element.76, bf16[6,64,64,48]{2,3,1,0:T(8,128)(2,1)} %fusion.18, bf16[6,3,64,48]{2,3,0,1:T(8,128)(2,1)} %copy-done.2), kind=kOutput, calls=%fused_computation.15 | convolution fusion | flops 115900416 | bytes 15409670 | tf_op jit(solution)/shard_map/while/body/eval_jaxpr/hwie,hwy->hiye/dot_general | solution.py:89
  158.4 9.9 %copy.130 = f32[6,64,48,48]{3,2,1,0:T(8,128)} copy(f32[6,64,48,48]{1,2,3,0:T(8,128)} %add_bitcast_fusion.1) | data formatting | bytes 7077888 | tf_op jit(solution)/shard_map/while/body/eval_jaxpr/add | solution.py:99
  168.2 8.7 %stack.19 = f32[6,1,64,2304]{3,2,0,1:T(8,128)} reshape(f32[6,64,48,48]{3,2,1,0:T(8,128)} %copy.130) | data formatting | bytes 7077888 | tf_op jit(solution)/shard_map/while/body/eval_jaxpr/stack | solution.py:102
  176.9 11.8 %add_bitcast_fusion.2 = f32[6,64,48,48]{1,2,3,0:T(8,128)} fusion(f32[6,48,64,48]{2,1,3,0:T(8,128)} %fusion.12, pred[6]{0:T(512)(128)(4,1)S(1)} %get-tuple-element.75, pred[6]{0:T(512)(128)(4,1)S(1)} %get-tuple-element.72, bf16[6,64,64,48]{2,3,1,0:T(8,128)(2,1)} %fusion.18, bf16[6,3,64,48]{2,3,0,1:T(8,128)(2,1)} %copy-done.2), kind=kOutput, calls=%fused_computation.16 | convolution fusion | flops 115900416 | bytes 15409164 | tf_op jit(solution)/shard_map/while/body/eval_jaxpr/zixl,zxo->ziol/dot_general | solution.py:89
  188.7 9.9 %copy.127 = f32[6,64,48,48]{3,2,1,0:T(8,128)} copy(f32[6,64,48,48]{1,2,3,0:T(8,128)} %add_bitcast_fusion.2) | data formatting | bytes 7077888 | tf_op jit(solution)/shard_map/while/body/eval_jaxpr/add | solution.py:99
  198.6 8.5 %stack.18 = f32[6,1,64,2304]{3,2,0,1:T(8,128)} reshape(f32[6,64,48,48]{3,2,1,0:T(8,128)} %copy.127) | data formatting | bytes 7077888 | tf_op jit(solution)/shard_map/while/body/eval_jaxpr/stack | solution.py:102
  207.0 4.0 pad_maximum_fusion
  211.1 5.0 copy.134
  216.4 5.2 bitcast_select_fusion
  221.6 14.6 %fusion = f32[16,64,2304]{2,0,1:T(8,128)} fusion(f32[18,64,2304]{2,1,0:T(8,128)S(1)} %bitcast_select_fusion, s32[18]{0:T(128)S(1)} %eq.44), kind=kOutput, calls=%fused_computation.7 | convolution fusion | flops 509608224 | bytes 20054088 | tf_op jit(solution)/shard_map/while/body/eval_jaxpr/nk,kbc->nbc/dot_general | solution.py:120
  236.2 9.1 %copy.136 = f32[16,64,2304]{2,1,0:T(8,128)S(1)} copy(f32[16,64,2304]{2,0,1:T(8,128)} %fusion) | data formatting | bytes 18874368 | tf_op jit(solution)/shard_map/while/body/eval_jaxpr/nk,kbc->nbc/dot_general | solution.py:120
  245.3 4.6 copy.137
  250.0 27.1 %reduce-scatter.4.cloned.1.call-done = f32[32,16,2304]{2,1,0:T(8,128)} async-done(((f32[64,16,2304]{2,1,0:T(8,128)}), f32[32,16,2304]{2,1,0:T(8,128)}) %reduce-scatter.4.cloned.1.call-update) | async-done | bytes 4718608 | tf_op jit(solution)/shard_map/reduce_scatter | solution.py:24
  277.2 56.9 %reduce-scatter.6.cloned.1.call-done = f32[8,16,2304]{2,1,0:T(8,128)} async-done(((f32[32,16,2304]{2,1,0:T(8,128)}), f32[8,16,2304]{2,1,0:T(8,128)}) %reduce-scatter.6.cloned.1.call-update) | async-done | bytes 1179664 | tf_op jit(solution)/shard_map/reduce_scatter | solution.py:24
  334.2 37.1 %reduce-scatter.8.cloned.1.call-done = f32[1,16,2304]{2,1,0:T(8,128)} async-done(((f32[8,16,2304]{2,1,0:T(8,128)}), f32[1,16,2304]{2,1,0:T(8,128)}) %reduce-scatter.8.cloned.1.call-update) | async-done | bytes 147472 | tf_op jit(solution)/shard_map/reduce_scatter | solution.py:24
  371.3 1.0 reshape_squeeze.3
  372.3 8.8 %all_to_all.5 = f32[4,4,2304]{2,1,0:T(4,128)S(1)} all-to-all(f32[4,4,2304]{2,1,0:T(4,128)S(1)} %reshape_squeeze.3), channel_id=1, replica_groups=mesh['gx_0'=4,'gx_1'=2,'gy'=8,'gz'=4] {'gz'}, dimensions={0} | all-to-all | bytes 294912 | tf_op jit(solution)/shard_map/all_to_all | solution.py:41
  381.3 0.7 reshape.202
  382.2 118.9 %all-gather.3.cloned.1.call-done = bf16[256,4,2304]{2,1,0:T(4,128)(2,1)} async-done(((bf16[1,4,2304]{2,1,0:T(4,128)(2,1)}), bf16[256,4,2304]{2,1,0:T(4,128)(2,1)}) %all-gather.3.cloned.1.call-update) | async-done | bytes 4718608 | tf_op jit(solution)/shard_map/all_gather | solution.py:141
  501.1 8.4 %reshape.203 = bf16[1024,2304]{1,0:T(8,128)(2,1)} reshape(bf16[256,4,2304]{2,1,0:T(4,128)(2,1)} %all-gather.3.cloned.1.call-done) | data formatting | bytes 9437184
  509.6 4.3 convolution_multiply_fusion
  (61 shorter events, 1.8 us)
Async XLA Ops:
  6.5 270.6 %reduce-scatter.4.cloned.1.call-start = ((), (), s32[]{:S(2)}) async-start(), calls=%async_computation.4 | async-start | bytes 14155776 | tf_op jit(solution)/shard_map/reduce_scatter | solution.py:24
  65.4 15.2 %copy-start.3 = (bf16[1024,48]{0,1:T(8,128)(2,1)S(1)}, bf16[1024,48]{0,1:T(8,128)(2,1)}, u32[]{:S(2)}) copy-start(bf16[1024,48]{0,1:T(8,128)(2,1)} %param.25) | copy-start | bytes 294916
  81.6 4.4 slice-start
  81.7 45.7 %copy-start.2 = (bf16[6,3,64,48]{2,3,0,1:T(8,128)(2,1)}, bf16[6,3,64,48]{2,3,0,1:T(8,128)(2,1)S(1)}, u32[]{:S(2)}) copy-start(bf16[6,3,64,48]{2,3,0,1:T(8,128)(2,1)S(1)} %copy_select_fusion) | copy-start | bytes 331780
  81.7 4.7 slice-start.1
  105.0 8.4 %copy-start.8 = (s32[3]{0:T(128)S(1)}, s32[3]{0:T(128)}, u32[]{:S(2)}) copy-start(s32[3]{0:T(128)} %constant.88) | copy-start | bytes 40
  105.0 8.4 %copy-start.1 = (s32[6,3]{0,1:T(4,128)S(1)}, s32[6,3]{0,1:T(4,128)}, u32[]{:S(2)}) copy-start(s32[6,3]{0,1:T(4,128)} %param.24) | copy-start | bytes 220
  105.0 9.6 %copy-start.7 = (s32[3]{0:T(128)S(1)}, s32[3]{0:T(128)}, u32[]{:S(2)}) copy-start(s32[3]{0:T(128)} %constant.91) | copy-start | bytes 40
  105.0 10.2 %copy-start.6 = (s32[3]{0:T(128)S(1)}, s32[3]{0:T(128)}, u32[]{:S(2)}) copy-start(s32[3]{0:T(128)} %constant.90) | copy-start | bytes 40
  105.0 10.7 %copy-start.5 = (s32[3]{0:T(128)S(1)}, s32[3]{0:T(128)}, u32[]{:S(2)}) copy-start(s32[3]{0:T(128)} %constant.89) | copy-start | bytes 40
  105.0 11.3 %copy-start.4 = (s32[3]{0:T(128)S(1)}, s32[3]{0:T(128)}, u32[]{:S(2)}) copy-start(s32[3]{0:T(128)} %constant.92) | copy-start | bytes 40
  113.4 14.0 %slice-start.2 = ((s8[4718592]{0:T(1024)(128)(4,1)}), s8[524288]{0:T(1024)(128)(4,1)S(1)}, s32[]{:S(2)}) async-start(s8[4718592]{0:T(1024)(128)(4,1)} %bitcast.83), calls=%async_computation.10 | async-start | bytes 1048576
  116.9 10.5 %slice-start.3 = ((s8[4718592]{0:T(1024)(128)(4,1)}), s8[4194304]{0:T(1024)(128)(4,1)S(1)}, s32[]{:S(2)}) async-start(s8[4718592]{0:T(1024)(128)(4,1)} %bitcast.83), calls=%async_computation.11 | async-start | bytes 8388608
  116.9 10.5 %copy-start = (f32[6,48,64,48]{2,1,3,0:T(8,128)S(1)}, f32[6,48,64,48]{2,1,3,0:T(8,128)}, u32[]{:S(2)}) copy-start(f32[6,48,64,48]{2,1,3,0:T(8,128)} %fusion.6) | copy-start | bytes 10616836
  250.0 84.1 %reduce-scatter.6.cloned.1.call-start = ((), (), s32[]{:S(2)}) async-start(), calls=%async_computation.5 | async-start | bytes 5898240 | tf_op jit(solution)/shard_map/reduce_scatter | solution.py:24
  277.1 94.2 %reduce-scatter.8.cloned.1.call-start = ((), (), s32[]{:S(2)}) async-start(), calls=%async_computation.6 | async-start | bytes 1327104 | tf_op jit(solution)/shard_map/reduce_scatter | solution.py:24
  334.1 167.0 %all-gather.3.cloned.1.call-start = ((), (), s32[]{:S(2)}) async-start(), calls=%async_computation.7 | async-start | bytes 4737024 | tf_op jit(solution)/shard_map/all_gather | solution.py:141
Sparse Core Ops, SparseCore 0:
  250.1 26.9 reduce-scatter.3
  279.6 54.4 reduce-scatter.5
  336.6 34.6 reduce-scatter.7
  382.2 118.8 all-gather.2
where the time goes:
time: 531 us; the launch traced here: 521 us
  waiting for transfers between devices  240 us (45%)
  local copies, waits for them, and re-layouts  119 us (22%)
  matrix products  85.9 us (16%)
  other arithmetic  52.9 us (10%)
  between operations  13.9 us (3%)
  blocking collectives  8.82 us (2%)
    reduce_scatter x3, waiting for transfers between devices, reduced_to_own(): pieces = lax.psum_scatter(pieces, axes[k], scatter_dimension=0, tiled=True)  121 us
    all_gather x1, waiting for transfers between devices, local(): lax.all_gather(rounded, GX_GY_GZ, axis=0, tiled=True)  119 us
    dot_general x6, matrix products, slot_terms(): jnp.einsum(contraction_form, reduced[last_slot], factors[middle_slot_inde...  47 us
    add x3, local copies, waits for them, and re-layouts, slot_terms(): by_row[row_slot_index]  29.6 us
    another operation x4, local copies, waits for them, and re-layouts, slot_terms(): stacked = jnp.stack(by_row, axis=1)  29.2 us
    select_n x2, other arithmetic, unpack(): unpacked = jnp.where(same_back, order_back(unpacked), unpacked)  28.6 us
    dot_general x3, matrix products, slot_terms(): jnp.einsum(REDUCE_FORMS[slot_pos], unpacked, factors[slot_pos], preferred...  20 us
    reshape x2, local copies, waits for them, and re-layouts, unpack(): unpacked = stored.reshape(number, extent, extent, extent)  19.2 us
  transfers between devices with their start and end apart: 4, of which 4 were waited for; matrix products, arithmetic and copies ran while one was open for 0% of the time, Pallas kernels for 0%

commit v1 on v0

v1 whole, which is shorter than its diff:
```python
import jax
import jax.numpy as jnp
from jax import lax
from jax.experimental import pallas as pl
from jax.experimental.pallas import tpu as pltpu
from jax.sharding import Mesh
from jax.sharding import PartitionSpec as P

N, NB, R, BS = 1024, 16, 48, 64
PITCH = 56
PQ = 1536


def turned(tile):
    return pltpu.roll(tile, BS, 1)


def contract_kernel(own, blk, ut, keep, send, sbuf, vv, ww, acc):
    slot = pl.program_id(0)
    slots = pl.num_programs(0)

    @pl.when(slot == 0)
    def _():
        def clear(t, carry):
            acc[t] = jnp.zeros((R * R, 128), jnp.float32)
            return carry

        lax.fori_loop(0, 8, clear, 0)

    i, j, k = own[slot * 3], own[slot * 3 + 1], own[slot * 3 + 2]

    @pl.when(i >= 0)
    def _():
        low = lax.broadcasted_iota(jnp.int32, (R, 128), 1) < BS
        halves = lax.broadcasted_iota(jnp.int32, (R, 128), 1) >> 6
        sbuf[...] = blk[0]

        @pl.when((i == j) | (j == k))
        def _():
            front, back = i == j, j == k

            def weigh(c, carry):
                at = pl.ds(pl.multiple_of(c * 128, 128), 128)
                lane = lax.broadcasted_iota(jnp.int32, (BS, 128), 1)
                x = lax.broadcasted_iota(jnp.int32, (BS, 128), 0)
                y = 2 * c + (lane >> 6)
                z = lane & 63
                f1 = jnp.where(x < y, 1.0, jnp.where(x == y, 0.5, 0.0))
                f2 = jnp.where(y < z, 1.0, jnp.where(y == z, 0.5, 0.0))
                f1 = jnp.where(front, f1, 1.0)
                f2 = jnp.where(back, f2, 1.0)
                f = f1 * f2
                f = jnp.where(f == 0.25, 1.0 / 6.0, f)
                sbuf[:, at] = (blk[0, :, at].astype(jnp.float32) * f).astype(jnp.bfloat16)
                return carry

            lax.fori_loop(0, 32, weigh, 0)

        ui, uj, uk = ut[i], ut[j], ut[k]
        ukz = jnp.concatenate([uk, jnp.zeros((R, BS), jnp.bfloat16)], axis=1)

        for c in range(8):
            v = jnp.dot(ui, sbuf[:, c * 512 : (c + 1) * 512], preferred_element_type=jnp.float32)
            for t in range(4):
                tile = v[:, t * 128 : (t + 1) * 128]
                other = turned(tile)
                y = 2 * (4 * c + t)
                vv[y * PITCH : y * PITCH + R, :] = jnp.where(low, tile, other)
                vv[(y + 1) * PITCH : (y + 1) * PITCH + R, :] = jnp.where(low, other, tile)
        for c in range(16):
            both = jnp.concatenate(
                [sbuf[:, c * 128 : (c + 1) * 128], sbuf[:, (c + 16) * 128 : (c + 17) * 128]], axis=0
            ).T
            both = jnp.concatenate([both[:BS], both[BS:]], axis=1)
            v = jnp.dot(uk, both, preferred_element_type=jnp.float32)
            for t in range(2):
                tile = v[:, t * 128 : (t + 1) * 128]
                other = turned(tile)
                y = 2 * c + t
                ww[y * PITCH : y * PITCH + R, :] = jnp.where(low, tile, other)
                ww[(y + 32) * PITCH : (y + 32) * PITCH + R, :] = jnp.where(low, other, tile)

        keep_i = halves == (i & 1)
        keep_j = halves == (j & 1)
        keep_k = halves == (k & 1)

        def add(row_block, keep, first, tile):
            at = pl.ds(first * R, R)
            acc[row_block >> 1, at, :] += jnp.where(keep, tile, 0.0)

        for g in range(12):
            parts = [
                vv[pl.ds(4 * g + t, BS, stride=PITCH), :].astype(jnp.bfloat16) for t in range(4)
            ]
            zk = jnp.dot(uj, jnp.concatenate(parts, axis=1), preferred_element_type=jnp.float32)
            zj = lax.dot_general(
                ukz,
                jnp.concatenate(parts, axis=0),
                (((1,), (1,)), ((), ())),
                preferred_element_type=jnp.float32,
            )
            for t in range(4):
                add(k, keep_k, 4 * g + t, zk[:, t * 128 : (t + 1) * 128])
            for t in range(2):
                tile = zj[:, t * 128 : (t + 1) * 128]
                other = turned(tile)
                add(j, keep_j, 4 * g + 2 * t, jnp.where(low, tile, other))
                add(j, keep_j, 4 * g + 2 * t + 1, jnp.where(low, other, tile))
            parts = [
                ww[pl.ds(4 * g + t, BS, stride=PITCH), :].astype(jnp.bfloat16) for t in range(4)
            ]
            zi = jnp.dot(uj, jnp.concatenate(parts, axis=1), preferred_element_type=jnp.float32)
            for t in range(4):
                add(i, keep_i, 4 * g + t, zi[:, t * 128 : (t + 1) * 128])

    @pl.when(slot == slots - 1)
    def _():
        core = lax.axis_index("gx_1")

        def pack(y, carry):
            for out, t in ((keep, 2 * y + core), (send, 2 * y + 1 - core)):
                at = 0
                for p in range(R):
                    first = p // 16 * 16
                    rows = R - first
                    plain = acc[t, p * R + first : (p + 1) * R, :]
                    swapped = acc.at[t][pl.ds(first * R + p, rows, stride=R), :]
                    out[y, at : at + rows, :] = (plain + swapped).astype(out.dtype)
                    at += rows
            return carry

        lax.fori_loop(0, 4, pack, 0)


def local_terms(blocks, ownership, basis_t):
    slots = blocks.shape[0]
    return pl.pallas_call(
        contract_kernel,
        grid_spec=pltpu.PrefetchScalarGridSpec(
            num_scalar_prefetch=1,
            grid=(slots,),
            in_specs=[
                pl.BlockSpec((1, BS, BS * BS), lambda s, own: (s, 0, 0)),
                pl.BlockSpec((NB, R, BS), lambda s, own: (0, 0, 0)),
            ],
            out_specs=[pl.BlockSpec((4, PQ, 128), lambda s, own: (0, 0, 0))] * 2,
            scratch_shapes=[
                pltpu.VMEM((BS, BS * BS), jnp.bfloat16),
                pltpu.VMEM((BS * PITCH, 128), jnp.float32),
                pltpu.VMEM((BS * PITCH, 128), jnp.float32),
                pltpu.VMEM((8, R * R, 128), jnp.float32),
            ],
        ),
        out_shape=[
            jax.ShapeDtypeStruct((4, PQ, 128), jnp.float32),
            jax.ShapeDtypeStruct((4, PQ, 128), jnp.bfloat16),
        ],
        compiler_params=pltpu.CompilerParams(
            dimension_semantics=("arbitrary",), vmem_limit_bytes=48 * 1024 * 1024
        ),
        name="contract",
    )(ownership.reshape(-1), blocks, basis_t)


MESH = pl.DeviceIdType.MESH
NY, NC, NZ, NX = 4, 2, 8, 4
F32, BF16 = jnp.float32, jnp.bfloat16


def exchange_kernel(
    keep,
    give,
    out,
    r1,
    e,
    r2a,
    r2b,
    fa,
    fb,
    r3a,
    r3b,
    g,
    g32,
    r4,
    h,
    yg,
    pb,
    r6,
    s1,
    q1,
    s2a,
    q2a,
    s2b,
    q2b,
    s3a,
    q3a,
    s3b,
    q3b,
    s4,
    q4,
    s5,
    q5,
    s6,
    q6,
):
    y, c, z, x = (lax.axis_index(a) for a in ("gx_0", "gx_1", "gy", "gz"))
    me = (y * NC + c) * NX + x
    half = NZ // 2

    def at_y(v):
        return (v, c, z, x)

    def at_x(v):
        return (y, c, z, v)

    def at_z(v):
        return (y, c, v, x)

    def in_plane(p):
        return (p // (NC * NX), (p // NX) % NC, z, p % NX)

    def around(v, o, n):
        return lax.rem(v + o, n)

    def remote(src, dst, send, recv, where):
        return pltpu.make_async_remote_copy(
            src_ref=src, dst_ref=dst, send_sem=send, recv_sem=recv, device_id=where, device_id_type=MESH
        )

    barrier = pltpu.get_barrier_semaphore()

    def greet_plane(o, carry):
        pl.semaphore_signal(
            barrier, inc=1, device_id=in_plane(around(me, o, 32)), device_id_type=MESH
        )
        return carry

    def greet_z(o, carry):
        pl.semaphore_signal(barrier, inc=1, device_id=at_z(around(z, o, NZ)), device_id_type=MESH)
        return carry

    lax.fori_loop(1, 32, greet_plane, 0)
    lax.fori_loop(1, NZ, greet_z, 0)
    pl.semaphore_wait(barrier, 31 + NZ - 1)

    def swap(k):
        part = pl.ds(k * half, half)
        return remote(
            give.at[:, part], r1.at[:, part], s1.at[k], q1.at[k], (y, 1 - c, z, x)
        )

    for k in range(2):
        swap(k).start()

    def add_pair(v, k):
        def body(t, carry):
            zz = k * half + t
            e[v, zz] = (keep[v, zz] + r1[v, zz].astype(F32)).astype(BF16)
            return carry

        lax.fori_loop(0, half, body, 0)

    def send2a(o):
        v = around(y, o, NY)
        return remote(e.at[v, pl.ds(0, half)], r2a.at[y], s2a.at[v], q2a.at[y], at_y(v))

    def got2a(o):
        v = around(y, o, NY)
        return remote(e.at[v, pl.ds(0, half)], r2a.at[v], s2a.at[v], q2a.at[v], at_y(v))

    def send2b(o):
        v = around(x, o, NX)
        return remote(e.at[:, pl.ds(half, half), v], r2b.at[x], s2b.at[v], q2b.at[x], at_x(v))

    def got2b(o):
        v = around(x, o, NX)
        return remote(e.at[:, pl.ds(half, half), v], r2b.at[v], s2b.at[v], q2b.at[v], at_x(v))

    swap(0).wait_recv()
    for o in (2, 1, 3):
        add_pair(around(y, o, NY), 0)
        send2a(o).start()
    swap(1).wait_recv()

    def add_all(v, carry):
        add_pair(v, 1)
        return carry

    lax.fori_loop(0, NY, add_all, 0)
    for o in (2, 1, 3):
        send2b(o).start()

    def send3a(o):
        v = around(x, o, NX)
        return remote(fa.at[:, v], r3a.at[x], s3a.at[v], q3a.at[x], at_x(v))

    def got3a(o):
        v = around(x, o, NX)
        return remote(fa.at[:, v], r3a.at[v], s3a.at[v], q3a.at[v], at_x(v))

    def send3b(o):
        v = around(y, o, NY)
        return remote(fb.at[v], r3b.at[y], s3b.at[v], q3b.at[y], at_y(v))

    def got3b(o):
        v = around(y, o, NY)
        return remote(fb.at[v], r3b.at[v], s3b.at[v], q3b.at[v], at_y(v))

    for o in (1, 3, 2):
        got2a(o).wait_recv()

    def add_a(t, carry):
        total = keep[y, t] + r1[y, t].astype(F32)
        for o in (1, 2, 3):
            total += r2a[around(y, o, NY), t].astype(F32)
        fa[t] = total
        return carry

    lax.fori_loop(0, half, add_a, 0)
    for o in (2, 1, 3):
        send3a(o).start()
    for o in (1, 3, 2):
        got2b(o).wait_recv()

    def add_b(t, carry):
        v, zz = t // half, lax.rem(t, half)
        total = keep[v, half + zz, x] + r1[v, half + zz, x].astype(F32)
        for o in (1, 2, 3):
            total += r2b[around(x, o, NX), v, zz].astype(F32)
        fb[v, zz] = total
        return carry

    lax.fori_loop(0, NY * half, add_b, 0)
    for o in (2, 1, 3):
        send3b(o).start()

    for o in (1, 3, 2):
        got3a(o).wait_recv()
    for o in (1, 3, 2):
        got3b(o).wait_recv()

    def add_c(t, carry):
        total = fa[t, x]
        for o in (1, 2, 3):
            total += r3a[around(x, o, NX), t]
        g32[t] = total
        g[t] = total.astype(BF16)
        total = fb[y, t]
        for o in (1, 2, 3):
            total += r3b[around(y, o, NY), t]
        g32[half + t] = total
        g[half + t] = total.astype(BF16)
        return carry

    lax.fori_loop(0, half, add_c, 0)

    def send4(o):
        v = around(z, o, NZ)
        return remote(g.at[v], r4.at[z], s4.at[v], q4.at[z], at_z(v))

    def got4(o):
        v = around(z, o, NZ)
        return remote(g.at[v], r4.at[v], s4.at[v], q4.at[v], at_z(v))

    for o in (4, 3, 5, 2, 6, 1, 7):
        send4(o).start()
    total = g32[z]
    for o in (1, 7, 2, 6, 3, 5, 4):
        got4(o).wait_recv()
        total += r4[around(z, o, NZ)].astype(F32)
    rows = total.astype(BF16)
    h[...] = rows
    yg[me] = rows

    def send5(o):
        p = around(me, o, 32)
        return remote(h, yg.at[me], s5.at[p], q5.at[me], in_plane(p))

    def got5(o):
        p = around(me, o, 32)
        return remote(h, yg.at[p], s5.at[p], q5.at[p], in_plane(p))

    def start5(o, carry):
        send5(o).start()
        return carry

    def wait5(o, carry):
        got5(o).wait_recv()
        return carry

    lax.fori_loop(1, 32, start5, 0)
    lax.fori_loop(1, 32, wait5, 0)

    weighted = []
    for t in range(12):
        tile = z * 12 + t
        w = jnp.where(
            tile < 48,
            1.0 if t % 3 == 0 else 2.0,
            jnp.where(tile < 80, 1.0 if t % 2 == 0 else 2.0, 1.0),
        )
        rows = yg[(y * NC + c) * NX + t // 3, (t % 3) * 16 : (t % 3 + 1) * 16]
        weighted.append((rows.astype(F32) * w).astype(BF16))
    weighted = jnp.concatenate(weighted, axis=0)
    row = lax.broadcasted_iota(jnp.int32, (64, 128), 0)
    lane = lax.broadcasted_iota(jnp.int32, (64, 128), 1)
    chosen = ((row >> 3) * 16 + 4 * x + (row & 7) == lane) & ((row & 7) < 4)
    left = lax.dot_general(
        chosen.astype(F32).astype(BF16),
        weighted,
        (((1,), (1,)), ((), ())),
        preferred_element_type=F32,
    ).astype(BF16)
    for t in range(8):
        right = jnp.concatenate([yg[4 * t + v] for v in range(4)], axis=0)
        part = jnp.dot(left, right, preferred_element_type=F32)
        for v in range(NZ):
            pb[v, :, t * 128 : (t + 1) * 128] = part[8 * v : 8 * v + 4]

    def send6(o):
        v = around(z, o, NZ)
        return remote(pb.at[v], r6.at[z], s6.at[v], q6.at[z], at_z(v))

    def got6(o):
        v = around(z, o, NZ)
        return remote(pb.at[v], r6.at[v], s6.at[v], q6.at[v], at_z(v))

    for o in (4, 3, 5, 2, 6, 1, 7):
        send6(o).start()
    total = pb[z]
    for o in (1, 7, 2, 6, 3, 5, 4):
        got6(o).wait_recv()
        total += r6[around(z, o, NZ)]
    out[...] = total / R

    for k in range(2):
        swap(k).wait_send()
    for o in (1, 2, 3):
        send2a(o).wait_send()
        send2b(o).wait_send()
        send3a(o).wait_send()
        send3b(o).wait_send()
    for o in range(1, NZ):
        send4(o).wait_send()
        send6(o).wait_send()

    def end5(o, carry):
        send5(o).wait_send()
        return carry

    lax.fori_loop(1, 32, end5, 0)


def summed_gram(keep, give):
    keep, give = (v.reshape(NY, NZ, NX, R, 128) for v in (keep, give))
    dma = pltpu.SemaphoreType.DMA
    half = NZ // 2
    return pl.pallas_call(
        exchange_kernel,
        out_shape=jax.ShapeDtypeStruct((4, 1024), F32),
        in_specs=[pl.BlockSpec(memory_space=pltpu.VMEM)] * 2,
        out_specs=pl.BlockSpec(memory_space=pltpu.VMEM),
        scratch_shapes=[
            pltpu.VMEM((NY, NZ, NX, R, 128), BF16),
            pltpu.VMEM((NY, NZ, NX, R, 128), BF16),
            pltpu.VMEM((NY, half, NX, R, 128), BF16),
            pltpu.VMEM((NX, NY, half, R, 128), BF16),
            pltpu.VMEM((half, NX, R, 128), F32),
            pltpu.VMEM((NY, half, R, 128), F32),
            pltpu.VMEM((NX, half, R, 128), F32),
            pltpu.VMEM((NY, half, R, 128), F32),
            pltpu.VMEM((NZ, R, 128), BF16),
            pltpu.VMEM((NZ, R, 128), F32),
            pltpu.VMEM((NZ, R, 128), BF16),
            pltpu.VMEM((R, 128), BF16),
            pltpu.VMEM((32, R, 128), BF16),
            pltpu.VMEM((NZ, 4, 1024), F32),
            pltpu.VMEM((NZ, 4, 1024), F32),
            dma((2,)),
            dma((2,)),
            dma((NY,)),
            dma((NY,)),
            dma((NX,)),
            dma((NX,)),
            dma((NX,)),
            dma((NX,)),
            dma((NY,)),
            dma((NY,)),
            dma((NZ,)),
            dma((NZ,)),
            dma((32,)),
            dma((32,)),
            dma((NZ,)),
            dma((NZ,)),
        ],
        compiler_params=pltpu.CompilerParams(
            collective_id=0, has_side_effects=True, vmem_limit_bytes=40 * 1024 * 1024
        ),
        name="exchange",
    )(keep, give)

GX_GY_GZ = ("gx_0", "gx_1", "gy", "gz")


def local(blocks, ownership, basis_rows):
    basis_t = basis_rows.reshape(NB, BS, R).swapaxes(1, 2)
    return summed_gram(*local_terms(blocks, ownership, basis_t))


def solution(mesh):
    split = Mesh(
        mesh.devices.reshape(4, 2, mesh.shape["gy"], mesh.shape["gz"]), GX_GY_GZ
    )
    return jax.shard_map(
        local,
        mesh=split,
        in_specs=(P(GX_GY_GZ, None, None), P(GX_GY_GZ, None), P()),
        out_specs=P(GX_GY_GZ, None),
        check_vma=False,
    )
```

time: 531 us -> 67.6 us (0.13); the launches traced: 521 us -> 67.7 us
  waiting for transfers between devices: 240 us -> 0 us
  local copies, waits for them, and re-layouts: 119 us -> 2.6 us
  matrix products: 85.9 us -> 0 us
  Pallas kernels: 0 us -> 65.1 us
  other arithmetic: 52.9 us -> 0 us
  between operations: 13.9 us -> 0.03 us
  blocking collectives: 8.82 us -> 0 us
    reduce_scatter x3 -> x0, waiting for transfers between devices: 121 us -> none  [reduced_to_own(): pieces = lax.psum_scatter(pieces, axes[k], scatter_dimension=0, tiled=True)]
    all_gather x1 -> x0, waiting for transfers between devices: 119 us -> none  [local(): lax.all_gather(rounded, GX_GY_GZ, axis=0, tiled=True)]
    dot_general x11 -> x0, matrix products: 85.9 us -> none  [the longest x6 47 us: slot_terms(): jnp.einsum(contraction_form, reduced[last_slot], factors[middle_slot_inde...]
    pallas_call x0 -> x2, Pallas kernels: none -> 65.1 us  [the longest x1 51.7 us: summed_gram(): pl.pallas_call(exchange_kernel, out_shape=jax.ShapeDtypeStruct((4, 1024),...]
    select_n x5 -> x0, other arithmetic: 45.7 us -> none  [the longest x2 28.6 us: unpack(): unpacked = jnp.where(same_back, order_back(unpacked), unpacked)]
    another operation x6 -> x0, local copies, waits for them, and re-layouts: 30.2 us -> none  [the longest x4 29.2 us: slot_terms(): stacked = jnp.stack(by_row, axis=1)]
    add x3 -> x0, local copies, waits for them, and re-layouts: 29.6 us -> none  [slot_terms(): by_row[row_slot_index]]
    reshape x6 -> x3, local copies, waits for them, and re-layouts: 19.6 us -> 1.23 us  [the longest x2 1.15 us: local(): basis_t = basis_rows.reshape(NB, BS, R).swapaxes(1, 2)]
  transfers between devices with their start and end apart: 4 -> 0, of which waited for: 4 -> 0; matrix products, arithmetic and copies ran while one was open for 0% -> 0% of each run, Pallas kernels for 0% -> 0%
where the time goes in v1:
time: 67.6 us; the launch traced here: 67.7 us
  Pallas kernels  65.1 us (96%)
  local copies, waits for them, and re-layouts  2.6 us (4%)
    pallas_call x1, Pallas kernels, summed_gram(): pl.pallas_call(exchange_kernel, out_shape=jax.ShapeDtypeStruct((4, 1024),...  51.7 us
    pallas_call x1, Pallas kernels, local_terms(): pl.pallas_call(contract_kernel, grid_spec=pltpu.PrefetchScalarGridSpec(nu...  13.4 us
    unnamed x2, local copies, waits for them, and re-layouts  1.37 us

profile of v1, /device:TPU:1, one launch (start us, length us, event | category | flops | bytes accessed | tf_op | source)
XLA Modules:
  0.0 67.7 jit_solution(13138533344169610782)
XLA Ops:
  0.0 0.8 %copy.5 = s32[6,3]{1,0:T(8,128)S(1)} copy(s32[6,3]{0,1:T(4,128)} %param.4) | data formatting | bytes 144 | tf_op args[1]
  0.8 0.1 reshape.12.own
  0.8 1.1 %reshape.13 = bf16[16,64,48]{1,0,2:T(8,128)(2,1)S(1)} reshape(bf16[1024,48]{0,1:T(8,128)(2,1)} %param.5) | data formatting | bytes 196608 | tf_op jit(solution)/shard_map/reshape | solution.py:506
  1.9 0.1 copy.8
  2.0 13.4 %contract.1 = (f32[4,1536,128]{2,1,0:T(8,128)S(1)}, bf16[4,1536,128]{2,1,0:T(8,128)(2,1)S(1)}) custom-call(s32[18]{0:T(128)S(1)} %reshape.12.own, bf16[6,64,4096]{2,1,0:T(8,128)(2,1)} %blk.1, bf16[16,48,64]{2,1,0:T(8,128)(2,1)S(1)} %bitcast.9), custom_call_target="tpu_custom_call" | custom-call | tf_op jit(solution)/shard_map/contract/pallas_call | solution.py:137
  15.4 51.7 %exchange.1 = f32[4,1024]{1,0:T(4,128)S(1)} custom-call(f32[4,8,4,48,128]{4,3,2,1,0:T(8,128)S(1)} %bitcast.7, bf16[4,8,4,48,128]{4,3,2,1,0:T(8,128)(2,1)S(1)} %bitcast.8), custom_call_target="tpu_custom_call" | custom-call | tf_op jit(solution)/shard_map/exchange/pallas_call | solution.py:458
  67.1 0.6 copy.10

commit v2 on v1

--- a/solution.py
+++ b/solution.py
@@ -15,43 +15,96 @@
     return pltpu.roll(tile, BS, 1)
 
 
-def contract_kernel(own, blk, ut, keep, send, sbuf, vv, ww, acc):
-    slot = pl.program_id(0)
-    slots = pl.num_programs(0)
-
-    @pl.when(slot == 0)
-    def _():
-        def clear(t, carry):
-            acc[t] = jnp.zeros((R * R, 128), jnp.float32)
-            return carry
-
-        lax.fori_loop(0, 8, clear, 0)
-
-    i, j, k = own[slot * 3], own[slot * 3 + 1], own[slot * 3 + 2]
+def contract_kernel(owned, stored, factors, keep, send, own, basis, blk, small, sems, ut, sbuf, vv, ww, acc):
+    slots = stored.shape[0]
+
+    def fetch(s):
+        return pltpu.make_async_copy(stored.at[s], blk.at[s], sems.at[s])
+
+    own_copy = pltpu.make_async_copy(owned, own, small.at[0])
+    basis_copy = pltpu.make_async_copy(factors, basis, small.at[1])
+    own_copy.start()
+    basis_copy.start()
+    for s in range(slots):
+        fetch(s).start()
+
+    def clear(t, carry):
+        acc[t] = jnp.zeros(acc.shape[1:], jnp.float32)
+        return carry
+
+    lax.fori_loop(0, 8, clear, 0)
+    own_copy.wait()
+    basis_copy.wait()
+    for v in range(NB):
+        ut[v] = basis[:, v * BS : (v + 1) * BS]
+
+    def add_slot(slot, carry):
+        fetch(slot).wait()
+        contract_slot(own, blk.at[slot], ut, sbuf, vv, ww, acc, slot)
+        return carry
+
+    lax.fori_loop(0, slots, add_slot, 0)
+
+    core = lax.axis_index("gx_1")
+
+    def pack(y, carry):
+        for out, t in ((keep, 2 * y + core), (send, 2 * y + 1 - core)):
+            at = 0
+            for p in range(R):
+                first = p // 16 * 16
+                rows = R - first
+                plain = acc[t, p * PITCH + first : p * PITCH + R, :]
+                swapped = acc.at[t][pl.ds(first * PITCH + p, rows, stride=PITCH), :]
+                out[y, at : at + rows, :] = (plain + swapped).astype(out.dtype)
+                at += rows
+        return carry
+
+    lax.fori_loop(0, 4, pack, 0)
+
+
+def contract_slot(own, blk, ut, sbuf, vv, ww, acc, slot):
+    i, j, k = own[0, slot], own[1, slot], own[2, slot]
 
     @pl.when(i >= 0)
     def _():
         low = lax.broadcasted_iota(jnp.int32, (R, 128), 1) < BS
         halves = lax.broadcasted_iota(jnp.int32, (R, 128), 1) >> 6
-        sbuf[...] = blk[0]
-
-        @pl.when((i == j) | (j == k))
+        front, back = i == j, j == k
+        lane = lax.broadcasted_iota(jnp.int32, (BS, 128), 1)
+        x = lax.broadcasted_iota(jnp.int32, (BS, 128), 0)
+        upper, z = lane >> 6, lane & 63
+
+        @pl.when(~(front | back))
         def _():
-            front, back = i == j, j == k
-
+            sbuf[...] = blk[...]
+
+        @pl.when(front ^ back)
+        def _():
+            def halves_of(n):
+                return (0.5 * n.astype(jnp.float32) + 0.5).astype(jnp.bfloat16)
+
+            def least(equal):
+                shape = jnp.full((BS, 128), jnp.where(equal, 0.0, 1.0), jnp.float32)
+                return shape.astype(jnp.bfloat16)
+
+            xy, yz = halves_of(upper - x), halves_of(z - upper)
+            xy_least, yz_least = least(front), least(back)
+            one = jnp.ones((BS, 128), jnp.bfloat16)
+            for c in range(32):
+                f1 = jnp.minimum(jnp.maximum(xy + jnp.bfloat16(c), xy_least), one)
+                f2 = jnp.minimum(jnp.maximum(yz - jnp.bfloat16(c), yz_least), one)
+                sbuf[:, c * 128 : (c + 1) * 128] = blk[:, c * 128 : (c + 1) * 128] * (f1 * f2)
+
+        @pl.when(front & back)
+        def _():
             def weigh(c, carry):
                 at = pl.ds(pl.multiple_of(c * 128, 128), 128)
-                lane = lax.broadcasted_iota(jnp.int32, (BS, 128), 1)
-                x = lax.broadcasted_iota(jnp.int32, (BS, 128), 0)
-                y = 2 * c + (lane >> 6)
-                z = lane & 63
+                y = 2 * c + upper
                 f1 = jnp.where(x < y, 1.0, jnp.where(x == y, 0.5, 0.0))
                 f2 = jnp.where(y < z, 1.0, jnp.where(y == z, 0.5, 0.0))
-                f1 = jnp.where(front, f1, 1.0)
-                f2 = jnp.where(back, f2, 1.0)
                 f = f1 * f2
                 f = jnp.where(f == 0.25, 1.0 / 6.0, f)
-                sbuf[:, at] = (blk[0, :, at].astype(jnp.float32) * f).astype(jnp.bfloat16)
+                sbuf[:, at] = (blk[:, at].astype(jnp.float32) * f).astype(jnp.bfloat16)
                 return carry
 
             lax.fori_loop(0, 32, weigh, 0)
@@ -85,7 +138,7 @@
         keep_k = halves == (k & 1)
 
         def add(row_block, keep, first, tile):
-            at = pl.ds(first * R, R)
+            at = pl.ds(first * PITCH, R)
             acc[row_block >> 1, at, :] += jnp.where(keep, tile, 0.0)
 
         for g in range(12):
@@ -113,53 +166,36 @@
             for t in range(4):
                 add(i, keep_i, 4 * g + t, zi[:, t * 128 : (t + 1) * 128])
 
-    @pl.when(slot == slots - 1)
-    def _():
-        core = lax.axis_index("gx_1")
-
-        def pack(y, carry):
-            for out, t in ((keep, 2 * y + core), (send, 2 * y + 1 - core)):
-                at = 0
-                for p in range(R):
-                    first = p // 16 * 16
-                    rows = R - first
-                    plain = acc[t, p * R + first : (p + 1) * R, :]
-                    swapped = acc.at[t][pl.ds(first * R + p, rows, stride=R), :]
-                    out[y, at : at + rows, :] = (plain + swapped).astype(out.dtype)
-                    at += rows
-            return carry
-
-        lax.fori_loop(0, 4, pack, 0)
-
-
-def local_terms(blocks, ownership, basis_t):
+
+def local_terms(blocks, ownership, basis_rows):
     slots = blocks.shape[0]
     return pl.pallas_call(
         contract_kernel,
-        grid_spec=pltpu.PrefetchScalarGridSpec(
-            num_scalar_prefetch=1,
-            grid=(slots,),
-            in_specs=[
-                pl.BlockSpec((1, BS, BS * BS), lambda s, own: (s, 0, 0)),
-                pl.BlockSpec((NB, R, BS), lambda s, own: (0, 0, 0)),
-            ],
-            out_specs=[pl.BlockSpec((4, PQ, 128), lambda s, own: (0, 0, 0))] * 2,
-            scratch_shapes=[
-                pltpu.VMEM((BS, BS * BS), jnp.bfloat16),
-                pltpu.VMEM((BS * PITCH, 128), jnp.float32),
-                pltpu.VMEM((BS * PITCH, 128), jnp.float32),
-                pltpu.VMEM((8, R * R, 128), jnp.float32),
-            ],
-        ),
+        in_specs=[
+            pl.BlockSpec(memory_space=pltpu.HBM),
+            pl.BlockSpec(memory_space=pltpu.HBM),
+            pl.BlockSpec(memory_space=pltpu.HBM),
+        ],
+        out_specs=[pl.BlockSpec(memory_space=pltpu.VMEM)] * 2,
+        scratch_shapes=[
+            pltpu.SMEM((3, slots), jnp.int32),
+            pltpu.VMEM((R, N), jnp.bfloat16),
+            pltpu.VMEM((slots, BS, BS * BS), jnp.bfloat16),
+            pltpu.SemaphoreType.DMA((2,)),
+            pltpu.SemaphoreType.DMA((slots,)),
+            pltpu.VMEM((NB, R, BS), jnp.bfloat16),
+            pltpu.VMEM((BS, BS * BS), jnp.bfloat16),
+            pltpu.VMEM((BS * PITCH, 128), jnp.float32),
+            pltpu.VMEM((BS * PITCH, 128), jnp.float32),
+            pltpu.VMEM((8, R * PITCH, 128), jnp.float32),
+        ],
         out_shape=[
             jax.ShapeDtypeStruct((4, PQ, 128), jnp.float32),
             jax.ShapeDtypeStruct((4, PQ, 128), jnp.bfloat16),
         ],
-        compiler_params=pltpu.CompilerParams(
-            dimension_semantics=("arbitrary",), vmem_limit_bytes=48 * 1024 * 1024
-        ),
+        compiler_params=pltpu.CompilerParams(vmem_limit_bytes=48 * 1024 * 1024),
         name="contract",
-    )(ownership.reshape(-1), blocks, basis_t)
+    )(ownership.T, blocks, basis_rows.T)
 
 
 MESH = pl.DeviceIdType.MESH
@@ -503,8 +539,7 @@
 
 
 def local(blocks, ownership, basis_rows):
-    basis_t = basis_rows.reshape(NB, BS, R).swapaxes(1, 2)
-    return summed_gram(*local_terms(blocks, ownership, basis_t))
+    return summed_gram(*local_terms(blocks, ownership, basis_rows))
 
 
 def solution(mesh):

time: 67.6 us -> 63.8 us (0.944)
  Pallas kernels: 65.1 us -> 61.9 us
    pallas_call x1, Pallas kernels: 13.4 us -> 4.43 us  [local_terms(): pl.pallas_call(contract_kernel, in_specs=[pl.BlockSpec(memory_space=pltpu...]
    pallas_call x1, Pallas kernels: 51.7 us -> 57.5 us  [summed_gram(): pl.pallas_call(exchange_kernel, out_shape=jax.ShapeDtypeStruct((4, 1024),...]
    reshape x3 -> x0, local copies, waits for them, and re-layouts: 1.23 us -> none  [the longest x2 1.15 us: local(): basis_t = basis_rows.reshape(NB, BS, R).swapaxes(1, 2)]
    unnamed x2 -> x5, local copies, waits for them, and re-layouts: 1.37 us -> 2.18 us
where the time goes in v2:
time: 63.8 us; the launch traced here: 64.1 us
  Pallas kernels  61.9 us (97%)
  local copies, waits for them, and re-layouts  2.18 us (3%)
    pallas_call x1, Pallas kernels, summed_gram(): pl.pallas_call(exchange_kernel, out_shape=jax.ShapeDtypeStruct((4, 1024),...  57.5 us
    pallas_call x1, Pallas kernels, local_terms(): pl.pallas_call(contract_kernel, in_specs=[pl.BlockSpec(memory_space=pltpu...  4.43 us
    unnamed x5, local copies, waits for them, and re-layouts  2.18 us

profile of v2, /device:TPU:1, one launch (start us, length us, event | category | flops | bytes accessed | tf_op | source)
XLA Modules:
  0.0 64.1 jit_solution(7126609454647866984)
XLA Ops:
  0.0 0.0 copy-start
  0.0 0.9 %copy-done = bf16[1024,48]{0,1:T(8,128)(2,1)S(1)} copy-done((bf16[1024,48]{0,1:T(8,128)(2,1)S(1)}, bf16[1024,48]{0,1:T(8,128)(2,1)}, u32[]{:S(2)}) %copy-start) | copy-done | bytes 98328
  0.9 0.0 copy-start.1
  0.9 0.7 %copy-done.1 = s32[6,3]{0,1:T(4,128)S(1)} copy-done((s32[6,3]{0,1:T(4,128)S(1)}, s32[6,3]{0,1:T(4,128)}, u32[]{:S(2)}) %copy-start.1) | copy-done | bytes 96
  1.6 4.4 %contract.1 = (f32[4,1536,128]{2,1,0:T(8,128)S(1)}, bf16[4,1536,128]{2,1,0:T(8,128)(2,1)S(1)}) custom-call(s32[3,6]{1,0:T(4,128)S(1)} %bitcast.7, bf16[6,64,4096]{2,1,0:T(8,128)(2,1)} %stored.1, bf16[48,1024]{1,0:T(8,128)(2,1)S(1)} %bitcast.6), custom_call_target="tpu_custom_call" | custom-call | tf_op jit(solution)/shard_map/contract/pallas_call | solution.py:172
  6.0 57.5 %exchange.1 = f32[4,1024]{1,0:T(4,128)S(1)} custom-call(f32[4,8,4,48,128]{4,3,2,1,0:T(8,128)S(1)} %bitcast.4, bf16[4,8,4,48,128]{4,3,2,1,0:T(8,128)(2,1)S(1)} %bitcast.5), custom_call_target="tpu_custom_call" | custom-call | tf_op jit(solution)/shard_map/exchange/pallas_call | solution.py:494
  63.5 0.6 copy.5
Async XLA Ops:
  0.0 0.9 %copy-start = (bf16[1024,48]{0,1:T(8,128)(2,1)S(1)}, bf16[1024,48]{0,1:T(8,128)(2,1)}, u32[]{:S(2)}) copy-start(bf16[1024,48]{0,1:T(8,128)(2,1)} %param.5) | copy-start | bytes 294916
  0.9 0.7 %copy-start.1 = (s32[6,3]{0,1:T(4,128)S(1)}, s32[6,3]{0,1:T(4,128)}, u32[]{:S(2)}) copy-start(s32[6,3]{0,1:T(4,128)} %param.4) | copy-start | bytes 220

commit v3 on v2

v3 whole, which is shorter than its diff:
```python
import jax
import jax.numpy as jnp
from jax import lax
from jax.experimental import pallas as pl
from jax.experimental.pallas import tpu as pltpu
from jax.sharding import Mesh
from jax.sharding import PartitionSpec as P

N, NB, R, BS = 1024, 16, 48, 64
PITCH = 56
AB, DG = 1024, 256


def turned(tile):
    return pltpu.roll(tile, BS, 1)


def contract_kernel(
    owned, stored, factors, keep, keep_d, send, send_d, own, basis, blk, small, sems, ut, sbuf, vv, ww, acc
):
    slots = stored.shape[0]

    def fetch(s):
        return pltpu.make_async_copy(stored.at[s], blk.at[s], sems.at[s])

    own_copy = pltpu.make_async_copy(owned, own, small.at[0])
    basis_copy = pltpu.make_async_copy(factors, basis, small.at[1])
    own_copy.start()
    basis_copy.start()
    for s in range(slots):
        fetch(s).start()

    def clear(t, carry):
        acc[t] = jnp.zeros(acc.shape[1:], jnp.float32)
        return carry

    lax.fori_loop(0, 8, clear, 0)
    own_copy.wait()
    basis_copy.wait()
    for v in range(NB):
        ut[v] = basis[:, v * BS : (v + 1) * BS]

    def add_slot(slot, carry):
        fetch(slot).wait()
        contract_slot(own, blk.at[slot], ut, sbuf, vv, ww, acc, slot)
        return carry

    lax.fori_loop(0, slots, add_slot, 0)

    core = lax.axis_index("gx_1")

    def pack(y, carry):
        for out, out_d, t in ((keep, keep_d, 2 * y + core), (send, send_d, 2 * y + 1 - core)):

            def rows_of(p, first, count):
                plain = acc[t, p * PITCH + first : p * PITCH + first + count, :]
                swapped = acc.at[t][pl.ds(first * PITCH + p, count, stride=PITCH), :]
                return plain + swapped

            at = 0
            for p in range(0, R - 8, 2):
                first = p // 8 * 8 + 8
                both = [rows_of(v, first, R - first) for v in (p, p + 1)]
                both = jnp.concatenate(both, axis=0)
                out[y, at : at + both.shape[0], :] = both.astype(out.dtype)
                at += both.shape[0]
            rest = [
                2.0 * acc.at[t][pl.ds((16 * v + 8) * (PITCH + 1), 8, stride=PITCH + 1), :]
                for v in range(3)
            ]
            rest = jnp.concatenate(rest + [jnp.zeros((AB - at - 24, 128), jnp.float32)], axis=0)
            out[y, at:AB, :] = rest.astype(out.dtype)
            row = lax.broadcasted_iota(jnp.int32, (8, 128), 0)
            for v in range(3):
                for a in range(0, 8, 2):
                    both = []
                    for b in (a, a + 1):
                        upper = rows_of(16 * v + b, 16 * v, 8)
                        lower = rows_of(16 * v + 8 + b, 16 * v + 8, 8)
                        both.append(jnp.where(row >= b, upper, lower))
                    at = (8 * v + a) * 8
                    both = jnp.concatenate(both, axis=0)
                    out_d[y, at : at + 16, :] = both.astype(out.dtype)
            out_d[y, 192:, :] = jnp.zeros((64, 128), out.dtype)
        return carry

    lax.fori_loop(0, 4, pack, 0)


def contract_slot(own, blk, ut, sbuf, vv, ww, acc, slot):
    i, j, k = own[0, slot], own[1, slot], own[2, slot]

    @pl.when(i >= 0)
    def _():
        low = lax.broadcasted_iota(jnp.int32, (R, 128), 1) < BS
        halves = lax.broadcasted_iota(jnp.int32, (R, 128), 1) >> 6
        front, back = i == j, j == k
        lane = lax.broadcasted_iota(jnp.int32, (BS, 128), 1)
        x = lax.broadcasted_iota(jnp.int32, (BS, 128), 0)
        upper, z = lane >> 6, lane & 63

        @pl.when(~(front | back))
        def _():
            sbuf[...] = blk[...]

        @pl.when(front ^ back)
        def _():
            def halves_of(n):
                return (0.5 * n.astype(jnp.float32) + 0.5).astype(jnp.bfloat16)

            def least(equal):
                shape = jnp.full((BS, 128), jnp.where(equal, 0.0, 1.0), jnp.float32)
                return shape.astype(jnp.bfloat16)

            xy, yz = halves_of(upper - x), halves_of(z - upper)
            xy_least, yz_least = least(front), least(back)
            one = jnp.ones((BS, 128), jnp.bfloat16)
            for c in range(32):
                f1 = jnp.minimum(jnp.maximum(xy + jnp.bfloat16(c), xy_least), one)
                f2 = jnp.minimum(jnp.maximum(yz - jnp.bfloat16(c), yz_least), one)
                sbuf[:, c * 128 : (c + 1) * 128] = blk[:, c * 128 : (c + 1) * 128] * (f1 * f2)

        @pl.when(front & back)
        def _():
            def weigh(c, carry):
                at = pl.ds(pl.multiple_of(c * 128, 128), 128)
                y = 2 * c + upper
                f1 = jnp.where(x < y, 1.0, jnp.where(x == y, 0.5, 0.0))
                f2 = jnp.where(y < z, 1.0, jnp.where(y == z, 0.5, 0.0))
                f = f1 * f2
                f = jnp.where(f == 0.25, 1.0 / 6.0, f)
                sbuf[:, at] = (blk[:, at].astype(jnp.float32) * f).astype(jnp.bfloat16)
                return carry

            lax.fori_loop(0, 32, weigh, 0)

        ui, uj, uk = ut[i], ut[j], ut[k]
        ukz = jnp.concatenate([uk, jnp.zeros((R, BS), jnp.bfloat16)], axis=1)

        for c in range(8):
            v = jnp.dot(ui, sbuf[:, c * 512 : (c + 1) * 512], preferred_element_type=jnp.float32)
            for t in range(4):
                tile = v[:, t * 128 : (t + 1) * 128]
                other = turned(tile)
                y = 2 * (4 * c + t)
                vv[y * PITCH : y * PITCH + R, :] = jnp.where(low, tile, other)
                vv[(y + 1) * PITCH : (y + 1) * PITCH + R, :] = jnp.where(low, other, tile)
        for c in range(16):
            both = jnp.concatenate(
                [sbuf[:, c * 128 : (c + 1) * 128], sbuf[:, (c + 16) * 128 : (c + 17) * 128]], axis=0
            ).T
            both = jnp.concatenate([both[:BS], both[BS:]], axis=1)
            v = jnp.dot(uk, both, preferred_element_type=jnp.float32)
            for t in range(2):
                tile = v[:, t * 128 : (t + 1) * 128]
                other = turned(tile)
                y = 2 * c + t
                ww[y * PITCH : y * PITCH + R, :] = jnp.where(low, tile, other)
                ww[(y + 32) * PITCH : (y + 32) * PITCH + R, :] = jnp.where(low, other, tile)

        keep_i = halves == (i & 1)
        keep_j = halves == (j & 1)
        keep_k = halves == (k & 1)

        def add(row_block, keep, first, tile):
            at = pl.ds(first * PITCH, R)
            acc[row_block >> 1, at, :] += jnp.where(keep, tile, 0.0)

        for g in range(12):
            parts = [
                vv[pl.ds(4 * g + t, BS, stride=PITCH), :].astype(jnp.bfloat16) for t in range(4)
            ]
            zk = jnp.dot(uj, jnp.concatenate(parts, axis=1), preferred_element_type=jnp.float32)
            zj = lax.dot_general(
                ukz,
                jnp.concatenate(parts, axis=0),
                (((1,), (1,)), ((), ())),
                preferred_element_type=jnp.float32,
            )
            for t in range(4):
                add(k, keep_k, 4 * g + t, zk[:, t * 128 : (t + 1) * 128])
            for t in range(2):
                tile = zj[:, t * 128 : (t + 1) * 128]
                other = turned(tile)
                add(j, keep_j, 4 * g + 2 * t, jnp.where(low, tile, other))
                add(j, keep_j, 4 * g + 2 * t + 1, jnp.where(low, other, tile))
            parts = [
                ww[pl.ds(4 * g + t, BS, stride=PITCH), :].astype(jnp.bfloat16) for t in range(4)
            ]
            zi = jnp.dot(uj, jnp.concatenate(parts, axis=1), preferred_element_type=jnp.float32)
            for t in range(4):
                add(i, keep_i, 4 * g + t, zi[:, t * 128 : (t + 1) * 128])


def local_terms(blocks, ownership, basis_rows):
    slots = blocks.shape[0]
    return pl.pallas_call(
        contract_kernel,
        in_specs=[
            pl.BlockSpec(memory_space=pltpu.HBM),
            pl.BlockSpec(memory_space=pltpu.HBM),
            pl.BlockSpec(memory_space=pltpu.HBM),
        ],
        out_specs=[pl.BlockSpec(memory_space=pltpu.VMEM)] * 4,
        scratch_shapes=[
            pltpu.SMEM((3, slots), jnp.int32),
            pltpu.VMEM((R, N), jnp.bfloat16),
            pltpu.VMEM((slots, BS, BS * BS), jnp.bfloat16),
            pltpu.SemaphoreType.DMA((2,)),
            pltpu.SemaphoreType.DMA((slots,)),
            pltpu.VMEM((NB, R, BS), jnp.bfloat16),
            pltpu.VMEM((BS, BS * BS), jnp.bfloat16),
            pltpu.VMEM((BS * PITCH, 128), jnp.float32),
            pltpu.VMEM((BS * PITCH, 128), jnp.float32),
            pltpu.VMEM((8, R * PITCH, 128), jnp.float32),
        ],
        out_shape=[
            jax.ShapeDtypeStruct((4, AB, 128), jnp.float32),
            jax.ShapeDtypeStruct((4, DG, 128), jnp.float32),
            jax.ShapeDtypeStruct((4, AB, 128), jnp.bfloat16),
            jax.ShapeDtypeStruct((4, DG, 128), jnp.bfloat16),
        ],
        compiler_params=pltpu.CompilerParams(vmem_limit_bytes=48 * 1024 * 1024),
        name="contract",
    )(ownership.T, blocks, basis_rows.T)


MESH = pl.DeviceIdType.MESH
NY, NC, NZ, NX = 4, 2, 8, 4
HALF = NZ // 2
F32, BF16 = jnp.float32, jnp.bfloat16
T3, T6 = F32, F32
OFF4 = (2, 1, 3)
ON4 = (1, 3, 2)
OFF8 = (4, 3, 5, 2, 6, 1, 7)
ON8 = (1, 7, 2, 6, 3, 5, 4)


def exchange_kernel(
    keep,
    keep_d,
    give,
    give_d,
    out,
    r1,
    r1d,
    e,
    ed,
    r2a,
    r2b,
    r2d,
    fa,
    fb,
    fd,
    r3a,
    r3b,
    r3d,
    g,
    gd,
    r4,
    r4d,
    h,
    yg,
    pb,
    r6,
    own_a,
    own_b,
    s1,
    q1,
    s2a,
    q2a,
    s2b,
    q2b,
    s2d,
    q2d,
    s3a,
    q3a,
    s3b,
    q3b,
    s3d,
    q3d,
    s4,
    q4,
    s4d,
    q4d,
    s5,
    q5,
    s6,
    q6,
):
    y, c, z, x = (lax.axis_index(a) for a in ("gx_0", "gx_1", "gy", "gz"))
    me = (y * NC + c) * NX + x

    def at_y(v):
        return (v, c, z, x)

    def at_x(v):
        return (y, c, z, v)

    def at_z(v):
        return (y, c, v, x)

    def in_plane(p):
        return (p // (NC * NX), (p // NX) % NC, z, p % NX)

    def remote(src, dst, send, recv, where):
        return pltpu.make_async_remote_copy(
            src_ref=src, dst_ref=dst, send_sem=send, recv_sem=recv, device_id=where, device_id_type=MESH
        )

    def exchange(src_of, land, send, recv, own, n, where):
        def to(o):
            v = lax.rem(own + o, n)
            return remote(src_of(v), land.at[own], send.at[v], recv.at[own], where(v))

        def got(o):
            v = lax.rem(own + o, n)
            return remote(src_of(v), land.at[v], send.at[v], recv.at[v], where(v))

        return to, got

    def slot(own, o, n):
        return lax.rem(own + o, n)

    barrier = pltpu.get_barrier_semaphore()

    def greet_plane(o, carry):
        pl.semaphore_signal(
            barrier, inc=1, device_id=in_plane(lax.rem(me + o, 32)), device_id_type=MESH
        )
        return carry

    def greet_z(o, carry):
        pl.semaphore_signal(
            barrier, inc=1, device_id=at_z(lax.rem(z + o, NZ)), device_id_type=MESH
        )
        return carry

    lax.fori_loop(1, NZ, greet_z, 0)
    lax.fori_loop(1, 32, greet_plane, 0)
    pl.semaphore_wait(barrier, 31 + NZ - 1)

    other = (y, 1 - c, z, x)
    swap_a = remote(give.at[:, pl.ds(0, HALF)], r1.at[:, pl.ds(0, HALF)], s1.at[0], q1.at[0], other)
    swap_b = remote(
        give.at[:, pl.ds(HALF, HALF)], r1.at[:, pl.ds(HALF, HALF)], s1.at[1], q1.at[1], other
    )
    swap_d = remote(give_d, r1d, s1.at[2], q1.at[2], other)
    swap_a.start()
    swap_d.start()
    swap_b.start()

    to2a, got2a = exchange(
        lambda v: e.at[v, pl.ds(0, HALF)], r2a, s2a, q2a, y, NY, at_y
    )
    to2b, got2b = exchange(
        lambda v: e.at[:, pl.ds(HALF, HALF), v], r2b, s2b, q2b, x, NX, at_x
    )
    to2d, got2d = exchange(lambda v: ed.at[v], r2d, s2d, q2d, z, NZ, at_z)
    to3a, got3a = exchange(lambda v: fa.at[v], r3a, s3a, q3a, x, NX, at_x)
    to3b, got3b = exchange(lambda v: fb.at[v], r3b, s3b, q3b, y, NY, at_y)
    to3d, got3d = exchange(lambda v: fd.at[v], r3d, s3d, q3d, y, NY, at_y)
    to4, got4 = exchange(lambda v: g.at[v], r4, s4, q4, z, NZ, at_z)
    to4d, got4d = exchange(lambda v: gd.at[v], r4d, s4d, q4d, x, NX, at_x)
    to6, got6 = exchange(lambda v: pb.at[v], r6, s6, q6, z, NZ, at_z)

    def pair(v, zz):
        return keep[v, zz] + r1[v, zz].astype(F32)

    def pair_d(v, zz):
        return keep_d[v, zz] + r1d[v, zz].astype(F32)

    swap_a.wait_recv()
    for o in OFF4:
        v = slot(y, o, NY)

        def add_1a(t, carry):
            e[v, t] = pair(v, t).astype(BF16)
            return carry

        lax.fori_loop(0, HALF, add_1a, 0)
        to2a(o).start()
    swap_d.wait_recv()

    def add_1d(t, carry):
        for v in range(NY):
            ed[t, v] = pair_d(v, t).astype(BF16)
        return carry

    lax.fori_loop(0, NZ, add_1d, 0)
    for o in OFF8:
        to2d(o).start()
    swap_b.wait_recv()

    def add_1b(t, carry):
        v, zz = t // HALF, HALF + lax.rem(t, HALF)
        e[v, zz] = pair(v, zz).astype(BF16)
        return carry

    lax.fori_loop(0, NY * HALF, add_1b, 0)
    for o in OFF4:
        to2b(o).start()

    for o in ON4:
        got2a(o).wait_recv()

    def add_2a(t, carry):
        total = pair(y, t)
        for o in ON4:
            total += r2a[slot(y, o, NY), t].astype(F32)
        for v in range(NX):
            fa[v, t] = total[v].astype(T3)
        own_a[t] = total
        return carry

    lax.fori_loop(0, HALF, add_2a, 0)
    for o in OFF4:
        to3a(o).start()
    for o in ON4:
        got2b(o).wait_recv()

    def add_2b(t, carry):
        v, zz = t // HALF, lax.rem(t, HALF)
        total = keep[v, HALF + zz, x] + r1[v, HALF + zz, x].astype(F32)
        for o in ON4:
            total += r2b[slot(x, o, NX), v, zz].astype(F32)
        fb[v, zz] = total.astype(T3)
        own_b[v, zz] = total
        return carry

    lax.fori_loop(0, NY * HALF, add_2b, 0)
    for o in OFF4:
        to3b(o).start()
    for o in ON8:
        got2d(o).wait_recv()

    def add_2d(v, carry):
        total = pair_d(v, z)
        for o in ON8:
            total += r2d[slot(z, o, NZ), v].astype(F32)
        fd[v] = total
        return carry

    lax.fori_loop(0, NY, add_2d, 0)
    for o in OFF4:
        to3d(o).start()

    for o in ON4:
        got3a(o).wait_recv()
    mine = jnp.zeros((R - 16, 128), F32)

    def add_3a(t, mine):
        total = own_a[t, x]
        for o in ON4:
            total += r3a[slot(x, o, NX), t].astype(F32)
        g[t] = total.astype(BF16)
        return jnp.where(t == z, total, mine)

    mine = lax.fori_loop(0, HALF, add_3a, mine)
    for o in ON4:
        got3b(o).wait_recv()

    def add_3b(t, mine):
        total = own_b[y, t]
        for o in ON4:
            total += r3b[slot(y, o, NY), t].astype(F32)
        g[HALF + t] = total.astype(BF16)
        return jnp.where(HALF + t == z, total, mine)

    mine = lax.fori_loop(0, HALF, add_3b, mine)
    for o in OFF8:
        to4(o).start()
    for o in ON4:
        got3d(o).wait_recv()
    total = fd[y]
    for o in ON4:
        total += r3d[slot(y, o, NY)]
    for v in range(NX):
        gd[v] = total[8 * v : 8 * v + 8]
    for o in OFF4:
        to4d(o).start()
    for o in ON8:
        got4(o).wait_recv()
        mine += r4[slot(z, o, NZ)].astype(F32)
    total = gd[x]
    for o in ON4:
        got4d(o).wait_recv()
        total += r4d[slot(x, o, NX)]
    rows = jnp.concatenate([mine, total], axis=0).astype(BF16)
    h[...] = rows
    yg[me] = rows

    def send5(o):
        p = lax.rem(me + o, 32)
        return remote(h, yg.at[me], s5.at[p], q5.at[me], in_plane(p))

    def got5(o):
        p = lax.rem(me + o, 32)
        return remote(h, yg.at[p], s5.at[p], q5.at[p], in_plane(p))

    def start5(o, carry):
        send5(o).start()
        return carry

    def wait5(o, carry):
        got5(o).wait_recv()
        return carry

    lax.fori_loop(1, 32, start5, 0)
    lax.fori_loop(1, 32, wait5, 0)

    row = lax.broadcasted_iota(jnp.int32, (64, 128), 0)
    lane = lax.broadcasted_iota(jnp.int32, (64, 128), 1)
    chosen = ((row >> 3) * 16 + 4 * x + (row & 7) == lane) & ((row & 7) < 4)
    chosen = chosen.astype(F32).astype(BF16)
    line = lax.broadcasted_iota(jnp.int32, (40, 128), 0)
    parts = []
    for v in range(NX):
        own_x = yg[(y * NC + c) * NX + v].astype(F32)
        chunk = z * NX + v
        plain = jnp.where(chunk < 30, 2.0, 1.0)
        diagonal = 32 + lax.rem(z, 2) * 4 + v
        weight = jnp.where(line < 32, plain, jnp.where(line == diagonal, 1.0, 2.0))
        left = lax.dot_general(
            chosen,
            (own_x * weight).astype(BF16),
            (((1,), (1,)), ((), ())),
            preferred_element_type=F32,
        ).astype(BF16)
        right = jnp.concatenate([yg[NX * t + v] for t in range(8)], axis=1)
        parts.append(jnp.dot(left, right, preferred_element_type=F32))
    part = (parts[0] + parts[1]) + (parts[2] + parts[3])
    for v in range(NZ):
        pb[v] = part[8 * v : 8 * v + 4].astype(T6)

    for o in OFF8:
        to6(o).start()
    total = pb[z].astype(F32)
    for o in ON8:
        got6(o).wait_recv()
        total += r6[slot(z, o, NZ)].astype(F32)
    out[...] = total / R

    swap_a.wait_send()
    swap_b.wait_send()
    swap_d.wait_send()
    for o in ON4:
        for to in (to2a, to2b, to3a, to3b, to3d, to4d):
            to(o).wait_send()
    for o in ON8:
        for to in (to2d, to4, to6):
            to(o).wait_send()

    def end5(o, carry):
        send5(o).wait_send()
        return carry

    lax.fori_loop(1, 32, end5, 0)


def summed_gram(keep, keep_d, give, give_d):
    keep, give = (v.reshape(NY, NZ, NX, 32, 128) for v in (keep, give))
    keep_d, give_d = (v.reshape(NY, NZ, 32, 128) for v in (keep_d, give_d))
    dma = pltpu.SemaphoreType.DMA
    vmem = pltpu.VMEM
    return pl.pallas_call(
        exchange_kernel,
        out_shape=jax.ShapeDtypeStruct((4, 1024), F32),
        in_specs=[pl.BlockSpec(memory_space=vmem)] * 4,
        out_specs=pl.BlockSpec(memory_space=vmem),
        scratch_shapes=[
            vmem((NY, NZ, NX, 32, 128), BF16),
            vmem((NY, NZ, 32, 128), BF16),
            vmem((NY, NZ, NX, 32, 128), BF16),
            vmem((NZ, NY, 32, 128), BF16),
            vmem((NY, HALF, NX, 32, 128), BF16),
            vmem((NX, NY, HALF, 32, 128), BF16),
            vmem((NZ, NY, 32, 128), BF16),
            vmem((NX, HALF, 32, 128), T3),
            vmem((NY, HALF, 32, 128), T3),
            vmem((NY, 32, 128), F32),
            vmem((NX, HALF, 32, 128), T3),
            vmem((NY, HALF, 32, 128), T3),
            vmem((NY, 32, 128), F32),
            vmem((NZ, 32, 128), BF16),
            vmem((NX, 8, 128), F32),
            vmem((NZ, 32, 128), BF16),
            vmem((NX, 8, 128), F32),
            vmem((40, 128), BF16),
            vmem((32, 40, 128), BF16),
            vmem((NZ, 4, 1024), T6),
            vmem((NZ, 4, 1024), T6),
            vmem((HALF, NX, 32, 128), F32),
            vmem((NY, HALF, 32, 128), F32),
        ]
        + [dma((3,))] * 2
        + [dma((NY,))] * 2
        + [dma((NX,))] * 2
        + [dma((NZ,))] * 2
        + [dma((NX,))] * 2
        + [dma((NY,))] * 4
        + [dma((NZ,))] * 2
        + [dma((NX,))] * 2
        + [dma((32,))] * 2
        + [dma((NZ,))] * 2,
        compiler_params=pltpu.CompilerParams(
            collective_id=0, has_side_effects=True, vmem_limit_bytes=40 * 1024 * 1024
        ),
        name="exchange",
    )(keep, keep_d, give, give_d)

GX_GY_GZ = ("gx_0", "gx_1", "gy", "gz")


def local(blocks, ownership, basis_rows):
    return summed_gram(*local_terms(blocks, ownership, basis_rows))


def solution(mesh):
    split = Mesh(
        mesh.devices.reshape(4, 2, mesh.shape["gy"], mesh.shape["gz"]), GX_GY_GZ
    )
    return jax.shard_map(
        local,
        mesh=split,
        in_specs=(P(GX_GY_GZ, None, None), P(GX_GY_GZ, None), P()),
        out_specs=P(GX_GY_GZ, None),
        check_vma=False,
    )
```

time: 63.8 us -> 59.9 us (0.939)
  Pallas kernels: 61.9 us -> 57.9 us
    pallas_call x1, Pallas kernels: 57.5 us -> 47 us  [summed_gram(): pl.pallas_call(exchange_kernel, out_shape=jax.ShapeDtypeStruct((4, 1024),...]
    pallas_call x1, Pallas kernels: 4.43 us -> 10.9 us  [local_terms(): pl.pallas_call(contract_kernel, in_specs=[pl.BlockSpec(memory_space=pltpu...]
where the time goes in v3:
time: 59.9 us; the launch traced here: 60.1 us
  Pallas kernels  57.9 us (97%)
  local copies, waits for them, and re-layouts  2.18 us (4%)
    pallas_call x1, Pallas kernels, summed_gram(): pl.pallas_call(exchange_kernel, out_shape=jax.ShapeDtypeStruct((4, 1024),...  47 us
    pallas_call x1, Pallas kernels, local_terms(): pl.pallas_call(contract_kernel, in_specs=[pl.BlockSpec(memory_space=pltpu...  10.9 us
    unnamed x5, local copies, waits for them, and re-layouts  2.18 us

profile of v3, /device:TPU:1, one launch (start us, length us, event | category | flops | bytes accessed | tf_op | source)
XLA Modules:
  0.0 60.1 jit_solution(2701140922745457858)
XLA Ops:
  0.0 0.0 copy-start
  0.0 0.9 %copy-done = bf16[1024,48]{0,1:T(8,128)(2,1)S(1)} copy-done((bf16[1024,48]{0,1:T(8,128)(2,1)S(1)}, bf16[1024,48]{0,1:T(8,128)(2,1)}, u32[]{:S(2)}) %copy-start) | copy-done | bytes 98328
  0.9 0.0 copy-start.1
  0.9 0.7 %copy-done.1 = s32[6,3]{0,1:T(4,128)S(1)} copy-done((s32[6,3]{0,1:T(4,128)S(1)}, s32[6,3]{0,1:T(4,128)}, u32[]{:S(2)}) %copy-start.1) | copy-done | bytes 96
  1.6 10.9 %contract.1 = (f32[4,1024,128]{2,1,0:T(8,128)S(1)}, f32[4,256,128]{2,1,0:T(8,128)S(1)}, bf16[4,1024,128]{2,1,0:T(8,128)(2,1)S(1)}, bf16[4,256,128]{2,1,0:T(8,128)(2,1)S(1)}) custom-call(s32[3,6]{1,0:T(4,128)S(1)} %bitcast.11, bf16[6,64,4096]{2,1,0:T(8,128)(2,1)} %stored.1, bf16[48,1024]{1,0:T(8,128)(2,1)S(1)} %bitcast.10), custom_call_target="tpu_custom_call" | custom-call | tf_op jit(solution)/shard_map/contract/pallas_call | solution.py:197
  12.5 47.0 %exchange.1 = f32[4,1024]{1,0:T(4,128)S(1)} custom-call(f32[4,8,4,32,128]{4,3,2,1,0:T(8,128)S(1)} %bitcast.6, f32[4,8,32,128]{3,2,1,0:T(8,128)S(1)} %bitcast.8, bf16[4,8,4,32,128]{4,3,2,1,0:T(8,128)(2,1)S(1)} %bitcast.7, bf16[4,8,32,128]{3,2,1,0:T(8,128)(2,1)S(1)} %bitcast.9), custom_call_target="tpu_custom_call" | custom-call | tf_op jit(solution)/shard_map/exchange/pallas_call | solution.py:566
  59.5 0.6 %copy.5 = f32[4,1024]{1,0:T(4,128)} copy(f32[4,1024]{1,0:T(4,128)S(1)} %exchange.1) | data formatting | bytes 32768
Async XLA Ops:
  0.0 0.9 %copy-start = (bf16[1024,48]{0,1:T(8,128)(2,1)S(1)}, bf16[1024,48]{0,1:T(8,128)(2,1)}, u32[]{:S(2)}) copy-start(bf16[1024,48]{0,1:T(8,128)(2,1)} %param.5) | copy-start | bytes 294916
  0.9 0.7 %copy-start.1 = (s32[6,3]{0,1:T(4,128)S(1)}, s32[6,3]{0,1:T(4,128)}, u32[]{:S(2)}) copy-start(s32[6,3]{0,1:T(4,128)} %param.4) | copy-start | bytes 220
